TPU v7x, 512 devices: a whole 4x8x8 slice. The times are simulated.
512 devices in a mesh: gx: 8 (over z_lo, core), gy: 8 (over y), gz: 8 (over x, z_hi).
Axes of the slice: x: 4, y: 8, z: 8 (z_hi: 2, z_lo: 4; z = z_hi * 4 + z_lo), core: 2. Of those that a mesh axis runs over, the one named last changes fastest.
Arguments:
- head_inputs: bfloat16 [131072, 2048], P(('gx', 'gy', 'gz')), may hold values from -6 to 6
- step_raw: float32 [131072, 32], P(('gx', 'gy', 'gz')), may hold values from -4 to 4
- state_in: bfloat16 [131072, 128], P(('gx', 'gy', 'gz')), may hold values from -0.119628906 to 0.119628906
- state_out: bfloat16 [131072, 128], P(('gx', 'gy', 'gz')), may hold values from -0.119628906 to 0.119628906
- decay_log: float32 [32], replicated, may hold values from -13.5 to -3
- step_bias: float32 [32], replicated, may hold values from -1 to 0.5
- skip_gain: float32 [32], replicated, may hold values from 0.5 to 1.5
- checkpoints: bfloat16 [512, 32, 64, 128], P(('gx', 'gy'), None, 'gz'), may hold values from -6 to 6
- out_grad: bfloat16 [131072, 2048], P(('gx', 'gy', 'gz')), may hold values from -6 to 6
Outputs:
- input_grad: bfloat16 [131072, 2048], P(('gx', 'gy', 'gz'))
- step_grad: float32 [131072, 32], P(('gx', 'gy', 'gz'))
- state_in_grad: float32 [131072, 128], P(('gx', 'gy', 'gz'))
- state_out_grad: float32 [131072, 128], P(('gx', 'gy', 'gz'))
- decay_log_grad: float32 [32], replicated
- step_bias_grad: float32 [32], replicated
- skip_gain_grad: float32 [32], replicated
All inputs are finite; a program needn't handle non-finite values.
Results may differ from a plain program's by a relative error of at most 0.00065.
Values may be sent and summed in bfloat16 or wider, within the bound.
A program may use at most 128 MiB of HBM per device.

v0:
```python
import jax
import jax.numpy as jnp
from jax import lax
from jax.sharding import Mesh
from jax.sharding import PartitionSpec as P

GZ = ("gz_0", "gz_1")
GX_GY = ("gx_0", "gx_1", "gy")
GX_GY_GZ = ("gx_0", "gx_1", "gy", "gz_0", "gz_1")
highest = lax.Precision.HIGHEST


def neutral_like(array, identity):
    return jax.tree.map(
        lambda a, e: jnp.broadcast_to(jnp.asarray(e, a.dtype), a.shape), array, identity
    )


def carried_in(array, axes, combine, identity):
    before = start = neutral_like(array, identity)
    so_far = array
    for axis in reversed(axes):
        length, index = (lax.axis_size(axis), lax.axis_index(axis))
        pieces = jax.tree.map(lambda part: lax.all_gather(part, axis), so_far)
        inside, so_far = (start, start)
        for k in reversed(range(length)):
            passed = k > index
            so_far = combine(so_far, jax.tree.map(lambda part: part[k], pieces))
            inside = jax.tree.map(lambda new, old: jnp.where(passed, new, old), so_far, inside)
        before = combine(inside, before)
    return before


def by_axis(array, axes):
    for axis in axes:
        array = lax.psum(array, axis)
    return array


def block_forward(inputs, raw, b_mat, scores, read, decay_log, bias, skip, start):
    step = jax.nn.softplus(raw + bias)
    cum = jnp.cumsum(step * -jnp.exp(decay_log), axis=0)
    length = inputs.shape[0]
    rows = lax.broadcasted_iota(jnp.int32, (length, length), 0)
    cols = lax.broadcasted_iota(jnp.int32, (length, length), 1)
    lower = rows >= cols
    ctrans = cum.T
    gap = ctrans[:, :, None] - ctrans[:, None, :]
    mix = jnp.where(lower, jnp.exp(jnp.where(lower, gap, 0.0)), 0.0) * scores * step.T[:, None, :]
    inner = jnp.einsum("hts,shp->thp", mix, inputs, precision=highest)
    carried = read * jnp.exp(cum)[:, :, None]
    result = inner + carried + skip[None, :, None] * inputs
    tail = jnp.exp(cum[-1][None, :] - cum) * step
    final = jnp.exp(cum[-1])[:, None, None] * start + jnp.einsum(
        "sh,shp,sn->hpn", tail, inputs, b_mat, precision=highest
    )
    return (result, final)


def span_forward(inputs, raw, b_mat, scores, read, decay_log, bias, skip, start):
    length, heads = raw.shape
    width = inputs.shape[1] // heads
    states = start.shape[2]
    block = min(8, heads)
    blocks = heads // block
    grouped = inputs.reshape(length, blocks, block, width).transpose(1, 0, 2, 3)
    read_g = read.reshape(length, blocks, block, width).transpose(1, 0, 2, 3)
    raw_g = raw.reshape(length, blocks, block).transpose(1, 0, 2)

    def one_block(items):
        return block_forward(
            items[0], items[1], b_mat, scores, items[2], items[3], items[4], items[5], items[6]
        )

    result, final = lax.map(
        one_block,
        (
            grouped,
            raw_g,
            read_g,
            decay_log.reshape(blocks, block),
            bias.reshape(blocks, block),
            skip.reshape(blocks, block),
            start.reshape(blocks, block, width, states),
        ),
    )
    result = result.transpose(1, 0, 2, 3).reshape(length, heads * width)
    return (result, final.reshape(heads, width, states))


def combine(earlier, later):
    return (earlier[0] * later[0], later[0][:, None, None] * earlier[1] + later[1])


def local(
    head_inputs,
    step_raw,
    state_in,
    state_out,
    decay_log,
    step_bias,
    skip_gain,
    checkpoints,
    out_grad,
):
    entering = lax.all_to_all(checkpoints, GZ, split_axis=0, concat_axis=2, tiled=True)[0]
    start = entering.astype(jnp.float32)
    length, heads = step_raw.shape
    width = head_inputs.shape[1] // heads
    states = state_in.shape[1]
    c_mat = state_out.astype(jnp.float32)
    b_mat = state_in.astype(jnp.float32)
    grad_rows = out_grad.astype(jnp.float32)
    step = jax.nn.softplus(step_raw + step_bias)
    cum = jnp.cumsum(step * -jnp.exp(decay_log), axis=0)
    weighted = (grad_rows.reshape(length, heads, width) * jnp.exp(cum)[:, :, None]).reshape(
        length, heads * width
    )
    local_term = jnp.dot(weighted.T, c_mat, precision=highest).reshape(heads, width, states)
    decays = jnp.exp(cum[-1])
    group = lax.axis_size(GZ)
    spread = jnp.broadcast_to(decays[None, :, None], (1, heads, group))
    got_decay, got_term = (
        lax.all_to_all(spread, GZ, split_axis=2, concat_axis=0, tiled=True),
        lax.all_to_all(local_term[None], GZ, split_axis=2, concat_axis=0, tiled=True),
    )
    got_decay = got_decay[:, :, 0]
    slice_width = got_term.shape[2]
    suffix_b = jnp.zeros((heads, slice_width, states), jnp.float32)
    suffix_a = jnp.ones((heads,), jnp.float32)
    inners = [None] * group
    leads = [None] * group
    for member in reversed(range(group)):
        inners[member] = suffix_b
        leads[member] = suffix_a
        suffix_b = got_term[member] + got_decay[member][:, None, None] * suffix_b
        suffix_a = got_decay[member] * suffix_a
    total = (suffix_a, suffix_b)
    neutral = (
        jnp.ones((heads,), jnp.float32),
        jnp.zeros((heads, slice_width, states), jnp.float32),
    )
    outer = carried_in(total, GX_GY, combine, neutral)
    carries = jnp.stack(
        [inners[member] + leads[member][:, None, None] * outer[1] for member in range(group)]
    )
    later = lax.all_to_all(carries, GZ, split_axis=0, concat_axis=2, tiled=True)[0]
    flat_start = entering.reshape(heads * width, states)
    scores = jnp.dot(state_out, state_in.T, preferred_element_type=jnp.float32)
    read = jnp.dot(state_out, flat_start.T, preferred_element_type=jnp.float32)
    _, pull = jax.vjp(
        span_forward,
        head_inputs.astype(jnp.float32),
        step_raw,
        b_mat,
        scores,
        read,
        decay_log,
        step_bias,
        skip_gain,
        start,
    )
    grads = pull((grad_rows, later))
    b_grad = grads[2] + jnp.dot(grads[3].T, c_mat, precision=highest)
    c_grad = jnp.dot(grads[3], b_mat, precision=highest) + jnp.dot(
        grads[4], flat_start.astype(jnp.float32), precision=highest
    )
    decay_sum, bias_sum, skip_sum = (
        by_axis(grads[5], GX_GY_GZ),
        by_axis(grads[6], GX_GY_GZ),
        by_axis(grads[7], GX_GY_GZ),
    )
    return (grads[0].astype(jnp.bfloat16), grads[1], b_grad, c_grad, decay_sum, bias_sum, skip_sum)


def solution(mesh):
    torus = Mesh(
        mesh.devices.reshape(4, 2, mesh.shape["gy"], 4, 2), ("gx_0", "gx_1", "gy", "gz_0", "gz_1")
    )
    return jax.shard_map(
        local,
        mesh=torus,
        in_specs=(
            P(GX_GY_GZ, None),
            P(GX_GY_GZ, None),
            P(GX_GY_GZ, None),
            P(GX_GY_GZ, None),
            P(),
            P(),
            P(),
            P(GX_GY, None, GZ, None),
            P(GX_GY_GZ, None),
        ),
        out_specs=(
            P(GX_GY_GZ, None),
            P(GX_GY_GZ, None),
            P(GX_GY_GZ, None),
            P(GX_GY_GZ, None),
            P(),
            P(),
            P(),
        ),
        check_vma=False,
    )
```

profile of v0, /device:TPU:64, one launch (start us, length us, event | category | flops | bytes accessed | tf_op | source)
XLA Modules:
  0.0 441.4 jit_solution(9832343445623595339)
XLA Ops:
  10.4 11.8 %all-to-all-start.1 = ((f32[1,32,8]{1,0,2:T(1,128)}), f32[1,32,8]{1,0,2:T(1,128)S(1)}, u32[]{:S(2)}, u32[]{:S(2)}) async-start(f32[1,32,8]{1,0,2:T(1,128)} %broadcast_in_dim.210), calls=%async_computation.1 | async-start | bytes 8192 | tf_op jit(solution)/shard_map/all_to_all | solution.py:124
  26.7 5.6 %all-to-all-done.1 = f32[1,32,8]{1,0,2:T(1,128)S(1)} async-done(((f32[1,32,8]{1,0,2:T(1,128)}), f32[1,32,8]{1,0,2:T(1,128)S(1)}, u32[]{:S(2)}, u32[]{:S(2)}) %all-to-all-start.1) | async-done | bytes 1056 | tf_op jit(solution)/shard_map/all_to_all | solution.py:124
  32.3 4.0 all-to-all-start
  37.5 29.1 %all-to-all-done = f32[1,32,64,128]{3,1,0,2:T(8,128)S(1)} async-done(((f32[1,32,64,128]{3,1,0,2:T(8,128)}), f32[1,32,64,128]{3,1,0,2:T(8,128)S(1)}, u32[]{:S(2)}, u32[]{:S(2)}) %all-to-all-start) | async-done | bytes 1048608 | tf_op jit(solution)/shard_map/all_to_all | solution.py:125
  68.3 4.2 all-to-all-start.3
  76.8 16.8 %all-gather = f32[8,1,32,1]{2,3,1,0:T(1,128)S(1)} all-gather(f32[1,1,32,1]{2,3,1,0:T(1,128)S(1)} %get-tuple-element.1868), channel_id=2, replica_groups=mesh['gx_0'=4,'gx_1'=2,'gy'=8,'gz_0'=4,'gz_1'=2] {'gy'}, dimensions={0}, use_global_device_ids=true | all-gather | bytes 1152 | tf_op jit(solution)/shard_map/all_gather | solution.py:24
  95.4 8.2 %all-gather.2 = f32[4,1,32]{2,1,0:T(1,128)S(1)} all-gather(f32[1,1,32]{2,1,0:T(1,128)S(1)} %get-tuple-element.1888), channel_id=1, replica_groups=mesh['gx_0'=4,'gx_1'=2,'gy'=8,'gz_0'=4,'gz_1'=2] {'gx_0'}, dimensions={0}, use_global_device_ids=true | all-gather | bytes 640 | tf_op jit(solution)/shard_map/all_gather | solution.py:24
  110.0 16.5 %all_gather.29 = f32[4,32,8,128]{3,2,1,0:T(8,128)S(1)} all-gather(f32[1,32,8,128]{3,2,1,0:T(8,128)S(1)} %slice_add_fusion.4), channel_id=1, replica_groups=mesh['gx_0'=4,'gx_1'=2,'gy'=8,'gz_0'=4,'gz_1'=2] {'gx_0'}, dimensions={0}, use_global_device_ids=true | all-gather | bytes 655360 | tf_op jit(solution)/shard_map/all_gather | solution.py:24
  134.1 6.5 %all-to-all-start.2 = ((f32[8,32,8,128]{3,2,1,0:T(8,128)}), f32[8,32,8,128]{3,2,1,0:T(8,128)}, u32[]{:S(2)}, u32[]{:S(2)}) async-start(f32[8,32,8,128]{3,2,1,0:T(8,128)} %constant_dynamic-update-slice_fusion.3), calls=%async_computation.2 | async-start | bytes 2097152 | tf_op jit(solution)/shard_map/all_to_all | solution.py:147
  145.8 57.4 %while.75 = (s32[]{:T(128)}, f32[4,256,8]{1,2,0:T(8,128)}, f32[4,8]{1,0:T(4,128)}, f32[4,1,8]{2,1,0:T(1,128)}, f32[4,256,8]{1,2,0:T(8,128)}, /*index=5*/f32[4,8,...) while((s32[]{:T(128)}, f32[4,256,8]{1,2,0:T(8,128)}, ...), condition=%wide.region_5.6_spmd.clone.clone, body=%wide.region_2.5_spmd.clone.clone.sunk | while | flops 3090474 | bytes 14180141 | solution.py:75
  147.4 4.2 multiply_dynamic-update-slice_fusion.4
  161.8 4.0 multiply_dynamic-update-slice_fusion.4
  176.1 4.2 multiply_dynamic-update-slice_fusion.4
  190.5 4.0 multiply_dynamic-update-slice_fusion.4
  216.8 157.2 %while.76 = (s32[]{:T(128)}, f32[256,256]{1,0:T(8,128)S(1)}, f32[256,128]{1,0:T(8,128)}, bf16[4,256,8,64]{1,3,2,0:T(8,128)(2,1)}, f32[4,256,8]{1,2,0:T(8,128)}, ...) while((s32[]{:T(128)}, f32[256,256]{1,0:T(8,128)S(1)}, ...), condition=%wide.region_19.20_spmd.clone.clone, body=%wide.region_6.19_spmd.clone.clone.sunk | while | flops 1215725568 | bytes 18326480 | solution.py:75
  222.0 6.5 %fusion.150 = (f32[8,256]{1,0:T(8,128)}, f32[8,256]{1,0:T(8,128)}, f32[256,256]{1,0:T(8,128)S(1)}, f32[8,256]{1,0:T(8,128)}) fusion(f32[4,8,256,256]{3,2,1,0:T(8,128)} %get-tuple-element.2474, s32[]{:T(128)S(6)} %sub.146, f32[256,256]{1,0:T(8,128)S(1)} %bitcast.579, f32[8,256]{1,0:T(8,128)S(1)} %dynamic-slice_bitcast_fusion.6, ...), kind=kOutput, calls=%fused_computation.87.clone.1 | convolution fusion | flops 408348672 | bytes 7964160 | tf_op jit(solution)/shard_map/transpose(jvp())/while/body/eval_jaxpr/hts,shp->thp/dot_general | solution.py:50
  233.7 3.2 reduce-window.62
  246.7 3.7 fusion.154
  261.3 6.5 %fusion.150 = (f32[8,256]{1,0:T(8,128)}, f32[8,256]{1,0:T(8,128)}, f32[256,256]{1,0:T(8,128)S(1)}, f32[8,256]{1,0:T(8,128)}) fusion(f32[4,8,256,256]{3,2,1,0:T(8,128)} %get-tuple-element.2474, s32[]{:T(128)S(6)} %sub.146, f32[256,256]{1,0:T(8,128)S(1)} %bitcast.579, f32[8,256]{1,0:T(8,128)S(1)} %dynamic-slice_bitcast_fusion.6, ...), kind=kOutput, calls=%fused_computation.87.clone.1 | convolution fusion | flops 408348672 | bytes 7964160 | tf_op jit(solution)/shard_map/transpose(jvp())/while/body/eval_jaxpr/hts,shp->thp/dot_general | solution.py:50
  273.0 3.2 reduce-window.62
  286.0 3.7 fusion.154
  292.5 2.8 fusion.151
  300.6 6.5 %fusion.150 = (f32[8,256]{1,0:T(8,128)}, f32[8,256]{1,0:T(8,128)}, f32[256,256]{1,0:T(8,128)S(1)}, f32[8,256]{1,0:T(8,128)}) fusion(f32[4,8,256,256]{3,2,1,0:T(8,128)} %get-tuple-element.2474, s32[]{:T(128)S(6)} %sub.146, f32[256,256]{1,0:T(8,128)S(1)} %bitcast.579, f32[8,256]{1,0:T(8,128)S(1)} %dynamic-slice_bitcast_fusion.6, ...), kind=kOutput, calls=%fused_computation.87.clone.1 | convolution fusion | flops 408348672 | bytes 7964160 | tf_op jit(solution)/shard_map/transpose(jvp())/while/body/eval_jaxpr/hts,shp->thp/dot_general | solution.py:50
  312.3 3.2 reduce-window.62
  325.3 3.7 fusion.154
  339.9 6.5 %fusion.150 = (f32[8,256]{1,0:T(8,128)}, f32[8,256]{1,0:T(8,128)}, f32[256,256]{1,0:T(8,128)S(1)}, f32[8,256]{1,0:T(8,128)}) fusion(f32[4,8,256,256]{3,2,1,0:T(8,128)} %get-tuple-element.2474, s32[]{:T(128)S(6)} %sub.146, f32[256,256]{1,0:T(8,128)S(1)} %bitcast.579, f32[8,256]{1,0:T(8,128)S(1)} %dynamic-slice_bitcast_fusion.6, ...), kind=kOutput, calls=%fused_computation.87.clone.1 | convolution fusion | flops 408348672 | bytes 7964160 | tf_op jit(solution)/shard_map/transpose(jvp())/while/body/eval_jaxpr/hts,shp->thp/dot_general | solution.py:50
  351.6 3.2 reduce-window.62
  364.6 3.7 fusion.154
  381.7 11.6 %all-reduce.4 = (f32[32]{0:T(128)S(1)}, f32[32]{0:T(128)S(1)}, f32[32]{0:T(128)S(1)}) all-reduce(f32[32]{0:T(128)S(1)} %reshape.895, f32[32]{0:T(128)S(1)} %reshape.896, f32[32]{0:T(128)S(1)} %reshape.897), channel_id=1, replica_groups=mesh['gx_0'=4,'gx_1'=2,'gy'=8,'gz_0'=4,'gz_1'=2] {'gx_0'}, use_global_device_ids=true, to_apply=%region_20.21 | all-reduce | flops 96 | bytes 768 | tf_op jit(solution)/shard_map/psum | solution.py:36
  395.8 16.1 %all-reduce.2 = (f32[32]{0:T(128)S(1)}, f32[32]{0:T(128)S(1)}, f32[32]{0:T(128)S(1)}) all-reduce(f32[32]{0:T(128)S(1)} %get-tuple-element.1825, f32[32]{0:T(128)S(1)} %get-tuple-element.1826, f32[32]{0:T(128)S(1)} %get-tuple-element.1827), channel_id=1, replica_groups=mesh['gx_0'=4,'gx_1'=2,'gy'=8,'gz_0'=4,'gz_1'=2] {'gy'}, use_global_device_ids=true, to_apply=%region_22.23 | all-reduce | flops 96 | bytes 768 | tf_op jit(solution)/shard_map/psum | solution.py:36
  411.8 10.9 %all-reduce.3 = (f32[32]{0:T(128)S(1)}, f32[32]{0:T(128)S(1)}, f32[32]{0:T(128)S(1)}) all-reduce(f32[32]{0:T(128)S(1)} %get-tuple-element.1813, f32[32]{0:T(128)S(1)} %get-tuple-element.1814, f32[32]{0:T(128)S(1)} %get-tuple-element.1815), channel_id=1, replica_groups=mesh['gx_0'=4,'gx_1'=2,'gy'=8,'gz_0'=4,'gz_1'=2] {'gz_0'}, use_global_device_ids=true, to_apply=%region_23.24 | all-reduce | flops 96 | bytes 768 | tf_op jit(solution)/shard_map/psum | solution.py:36
  422.8 9.3 %all-reduce.5 = (f32[32]{0:T(128)}, f32[32]{0:T(128)}, f32[32]{0:T(128)}) all-reduce(f32[32]{0:T(128)S(1)} %get-tuple-element.1816, f32[32]{0:T(128)S(1)} %get-tuple-element.1817, f32[32]{0:T(128)S(1)} %get-tuple-element.1818), channel_id=1, replica_groups=mesh['gx_0'=4,'gx_1'=2,'gy'=8,'gz_0'=4,'gz_1'=2] {'gz_1'}, use_global_device_ids=true, to_apply=%region_24.25 | all-reduce | flops 96 | bytes 768 | tf_op jit(solution)/shard_map/psum | solution.py:36
  (372 shorter events, 203.3 us)
Async XLA Ops:
  7.2 16.8 %copy-start = (bf16[256,128]{1,0:T(8,128)(2,1)S(1)}, bf16[256,128]{1,0:T(8,128)(2,1)}, u32[]{:S(2)}) copy-start(bf16[256,128]{1,0:T(8,128)(2,1)} %param.16) | copy-start | bytes 196612
  10.4 21.9 %all-to-all-start.1 = ((f32[1,32,8]{1,0,2:T(1,128)}), f32[1,32,8]{1,0,2:T(1,128)S(1)}, u32[]{:S(2)}, u32[]{:S(2)}) async-start(f32[1,32,8]{1,0,2:T(1,128)} %broadcast_in_dim.210), calls=%async_computation.1 | async-start | bytes 8192 | tf_op jit(solution)/shard_map/all_to_all | solution.py:124
  32.3 34.3 %all-to-all-start = ((f32[1,32,64,128]{3,1,0,2:T(8,128)}), f32[1,32,64,128]{3,1,0,2:T(8,128)S(1)}, u32[]{:S(2)}, u32[]{:S(2)}) async-start(f32[1,32,64,128]{3,1,0,2:T(8,128)} %copy.171), calls=%async_computation | async-start | bytes 2097152 | tf_op jit(solution)/shard_map/all_to_all | solution.py:125
  36.3 69.5 %all-gather.5.cloned.1.call-start = ((), (), s32[]{:S(2)}) async-start(), calls=%async_computation.4 | async-start | bytes 1179648 | tf_op jit(solution)/shard_map/all_gather | solution.py:24
  37.0 31.3 %copy-start.18 = (f32[32]{0:T(128)}, f32[32]{0:T(128)S(1)}, u32[]{:S(2)}) copy-start(f32[32]{0:T(128)S(1)} %get-tuple-element.1883) | copy-start | bytes 388
  37.4 30.9 %copy-start.20 = (f32[32]{0:T(128)}, f32[32]{0:T(128)S(1)}, u32[]{:S(2)}) copy-start(f32[32]{0:T(128)S(1)} %get-tuple-element.1874) | copy-start | bytes 388
  37.4 30.9 %copy-start.22 = (f32[32]{0:T(128)}, f32[32]{0:T(128)S(1)}, u32[]{:S(2)}) copy-start(f32[32]{0:T(128)S(1)} %get-tuple-element.1870) | copy-start | bytes 388
  37.4 30.9 %copy-start.24 = (f32[32]{0:T(128)}, f32[32]{0:T(128)S(1)}, u32[]{:S(2)}) copy-start(f32[32]{0:T(128)S(1)} %get-tuple-element.1872) | copy-start | bytes 388
  37.4 35.2 %copy-start.31 = (f32[32]{0:T(128)S(1)}, f32[32]{0:T(128)}, u32[]{:S(2)}) copy-start(f32[32]{0:T(128)} %param.18) | copy-start | bytes 388
  37.5 35.8 %copy-start.41 = (f32[32]{0:T(128)S(1)}, f32[32]{0:T(128)}, u32[]{:S(2)}) copy-start(f32[32]{0:T(128)} %param.17) | copy-start | bytes 388
  68.3 65.7 %all-to-all-start.3 = ((bf16[8,32,8,128]{3,2,1,0:T(8,128)(2,1)}), bf16[8,32,8,128]{3,2,1,0:T(8,128)(2,1)}, u32[]{:S(2)}, u32[]{:S(2)}) async-start(bf16[8,32,8,128]{3,2,1,0:T(8,128)(2,1)} %param.20), calls=%async_computation.3 | async-start | bytes 1048576 | tf_op jit(solution)/shard_map/all_to_all | solution.py:106
  93.6 14.0 %copy-start.15 = (f32[32]{0:T(128)}, f32[32]{0:T(128)S(1)}, u32[]{:S(2)}) copy-start(f32[32]{0:T(128)S(1)} %get-tuple-element.1879) | copy-start | bytes 388
  93.6 14.0 %copy-start.16 = (f32[32]{0:T(128)}, f32[32]{0:T(128)S(1)}, u32[]{:S(2)}) copy-start(f32[32]{0:T(128)S(1)} %get-tuple-element.1881) | copy-start | bytes 388
  95.4 14.4 %copy-start.21 = (f32[32]{0:T(128)}, f32[32]{0:T(128)S(1)}, u32[]{:S(2)}) copy-start(f32[32]{0:T(128)S(1)} %get-tuple-element.1889) | copy-start | bytes 388
  105.8 20.7 %copy-start.5 = (f32[8,32,8,128]{3,2,1,0:T(8,128)S(1)}, f32[8,32,8,128]{3,2,1,0:T(8,128)}, u32[]{:S(2)}) copy-start(f32[8,32,8,128]{3,2,1,0:T(8,128)} %all-gather.5.cloned.1.call-done) | copy-start | bytes 3145732
  105.8 20.7 %copy-start.33 = (f32[32]{0:T(128)S(1)}, f32[32]{0:T(128)}, u32[]{:S(2)}) copy-start(f32[32]{0:T(128)} %get-tuple-element.1844) | copy-start | bytes 388
  105.8 20.7 %copy-start.34 = (f32[32]{0:T(128)S(1)}, f32[32]{0:T(128)}, u32[]{:S(2)}) copy-start(f32[32]{0:T(128)} %get-tuple-element.1845) | copy-start | bytes 388
  105.8 20.7 %copy-start.35 = (f32[32]{0:T(128)S(1)}, f32[32]{0:T(128)}, u32[]{:S(2)}) copy-start(f32[32]{0:T(128)} %get-tuple-element.1884) | copy-start | bytes 388
  105.8 20.7 %copy-start.36 = (f32[32]{0:T(128)S(1)}, f32[32]{0:T(128)}, u32[]{:S(2)}) copy-start(f32[32]{0:T(128)} %get-tuple-element.1885) | copy-start | bytes 388
  105.8 20.7 %copy-start.37 = (f32[32]{0:T(128)S(1)}, f32[32]{0:T(128)}, u32[]{:S(2)}) copy-start(f32[32]{0:T(128)} %get-tuple-element.1886) | copy-start | bytes 388
  105.9 20.7 %copy-start.38 = (f32[32]{0:T(128)S(1)}, f32[32]{0:T(128)}, u32[]{:S(2)}) copy-start(f32[32]{0:T(128)} %get-tuple-element.1887) | copy-start | bytes 388
  107.6 21.2 %copy-start.30 = (f32[32]{0:T(128)S(1)}, f32[32]{0:T(128)}, u32[]{:S(2)}) copy-start(f32[32]{0:T(128)} %get-tuple-element.1839) | copy-start | bytes 388
  107.6 21.9 %copy-start.7 = (f32[1,32,8,128]{3,2,1,0:T(8,128)S(1)}, f32[1,32,8,128]{3,2,1,0:T(8,128)}, u32[]{:S(2)}) copy-start(f32[1,32,8,128]{3,2,1,0:T(8,128)} %get-tuple-element.1850) | copy-start | bytes 393220
  107.6 21.9 %copy-start.25 = (f32[32]{0:T(128)S(1)}, f32[32]{0:T(128)}, u32[]{:S(2)}) copy-start(f32[32]{0:T(128)} %copy-done.24) | copy-start | bytes 388
  107.7 21.9 %copy-start.40 = (f32[32]{0:T(128)S(1)}, f32[32]{0:T(128)}, u32[]{:S(2)}) copy-start(f32[32]{0:T(128)} %get-tuple-element.1840) | copy-start | bytes 388
  109.8 20.5 %copy-start.29 = (f32[32]{0:T(128)S(1)}, f32[32]{0:T(128)}, u32[]{:S(2)}) copy-start(f32[32]{0:T(128)} %get-tuple-element.1841) | copy-start | bytes 388
  109.9 21.2 %copy-start.6 = (f32[1,32,8,128]{3,2,1,0:T(8,128)S(1)}, f32[1,32,8,128]{3,2,1,0:T(8,128)}, u32[]{:S(2)}) copy-start(f32[1,32,8,128]{3,2,1,0:T(8,128)} %get-tuple-element.1851) | copy-start | bytes 393220
  109.9 21.1 %copy-start.23 = (f32[32]{0:T(128)S(1)}, f32[32]{0:T(128)}, u32[]{:S(2)}) copy-start(f32[32]{0:T(128)} %copy-done.22) | copy-start | bytes 388
  110.0 21.1 %copy-start.39 = (f32[32]{0:T(128)S(1)}, f32[32]{0:T(128)}, u32[]{:S(2)}) copy-start(f32[32]{0:T(128)} %get-tuple-element.1842) | copy-start | bytes 388
  134.1 76.5 %all-to-all-start.2 = ((f32[8,32,8,128]{3,2,1,0:T(8,128)}), f32[8,32,8,128]{3,2,1,0:T(8,128)}, u32[]{:S(2)}, u32[]{:S(2)}) async-start(f32[8,32,8,128]{3,2,1,0:T(8,128)} %constant_dynamic-update-slice_fusion.3), calls=%async_computation.2 | async-start | bytes 2097152 | tf_op jit(solution)/shard_map/all_to_all | solution.py:147
  374.0 58.1 %copy-start.2 = (f32[4,256,8,64]{1,3,2,0:T(8,128)S(1)}, f32[4,256,8,64]{1,3,2,0:T(8,128)}, u32[]{:S(2)}) copy-start(f32[4,256,8,64]{1,3,2,0:T(8,128)} %get-tuple-element.1033) | copy-start | bytes 6291460
  374.0 58.1 %copy-start.4 = (bf16[8,32,8,128]{3,2,0,1:T(8,128)(2,1)S(1)}, bf16[8,32,8,128]{3,2,0,1:T(8,128)(2,1)}, u32[]{:S(2)}) copy-start(bf16[8,32,8,128]{3,2,0,1:T(8,128)(2,1)} %copy-done.3) | copy-start | bytes 1572868
  (25 other events, 129.1 us)
Sparse Core Ops, SparseCore 0:
  68.4 37.3 all-gather.4
where the time goes:
time: 445 us; the launch traced here: 441 us
  local copies, waits for them, and re-layouts  99.1 us (22%)
  other arithmetic  98.9 us (22%)
  blocking collectives  95.8 us (22%)
  matrix products  70.4 us (16%)
  waiting for transfers between devices  35.7 us (8%)
  starting transfers between devices  26.6 us (6%)
  between operations  14.6 us (3%)
    psum x5, blocking collectives, by_axis(): array = lax.psum(array, axis)  50.4 us
    all_gather x5, blocking collectives, carried_in(): pieces = jax.tree.map(lambda part: lax.all_gather(part, axis), so_far)  45.4 us
    dot_general x8, matrix products, block_forward(): inner = jnp.einsum('hts,shp->thp', mix, inputs, precision=highest)  40.7 us
    dynamic_update_slice x36, local copies, waits for them, and re-layouts, span_forward(): lax.map(one_block, (grouped, raw_g, read_g, decay_log.reshape(blocks, blo...  32.7 us
    dynamic_update_slice x24, other arithmetic, span_forward(): lax.map(one_block, (grouped, raw_g, read_g, decay_log.reshape(blocks, blo...  30.3 us
    all_to_all x1, waiting for transfers between devices, local(): lax.all_to_all(local_term[None], GZ, split_axis=2, concat_axis=0, tiled=T...  29.1 us
    another operation x33, other arithmetic  27.8 us
    dot_general x8, matrix products, block_forward(): jnp.einsum('sh,shp,sn->hpn', tail, inputs, b_mat, precision=highest)  21.1 us
  transfers between devices with their start and end apart: 5, of which 3 were waited for; matrix products, arithmetic and copies ran while one was open for 20% of the time, Pallas kernels for 0%

commit v1 on v0

--- a/solution.py
+++ b/solution.py
@@ -33,7 +33,7 @@
 
 def by_axis(array, axes):
     for axis in axes:
-        array = lax.psum(array, axis)
+        array = jnp.sum(lax.all_gather(array, axis), axis=0)
     return array
 
 

time: 445 us -> 475 us (1.067)
  blocking collectives: 95.8 us -> 112 us
  local copies, waits for them, and re-layouts: 99.1 us -> 108 us
    psum x5 -> x0, blocking collectives: 50.4 us -> none  [by_axis(): array = lax.psum(array, axis)]
    unnamed x0 -> x4, blocking collectives: none -> 38.2 us
    all_gather x0 -> x3, blocking collectives: none -> 28.2 us  [by_axis(): array = jnp.sum(lax.all_gather(array, axis), axis=0)]
    unnamed x82 -> x113, local copies, waits for them, and re-layouts: 3.92 us -> 14.1 us
where the time goes in v1:
time: 475 us; the launch traced here: 471 us
  blocking collectives  112 us (24%)
  local copies, waits for them, and re-layouts  108 us (23%)
  other arithmetic  101 us (21%)
  matrix products  70.6 us (15%)
  waiting for transfers between devices  35.7 us (8%)
  starting transfers between devices  26.6 us (6%)
  between operations  17.3 us (4%)
    all_gather x5, blocking collectives, carried_in(): pieces = jax.tree.map(lambda part: lax.all_gather(part, axis), so_far)  45.4 us
    dot_general x8, matrix products, block_forward(): inner = jnp.einsum('hts,shp->thp', mix, inputs, precision=highest)  40.6 us
    unnamed x4, blocking collectives  38.2 us
    dynamic_update_slice x36, local copies, waits for them, and re-layouts, span_forward(): lax.map(one_block, (grouped, raw_g, read_g, decay_log.reshape(blocks, blo...  32.7 us
    dynamic_update_slice x24, other arithmetic, span_forward(): lax.map(one_block, (grouped, raw_g, read_g, decay_log.reshape(blocks, blo...  30.3 us
    all_to_all x1, waiting for transfers between devices, local(): lax.all_to_all(local_term[None], GZ, split_axis=2, concat_axis=0, tiled=T...  29.1 us
    all_gather x3, blocking collectives, by_axis(): array = jnp.sum(lax.all_gather(array, axis), axis=0)  28.2 us
    another operation x33, other arithmetic  27.8 us
  transfers between devices with their start and end apart: 5, of which 3 were waited for; matrix products, arithmetic and copies ran while one was open for 20% of the time, Pallas kernels for 0%

profile of v1, /device:TPU:64, one launch (start us, length us, event | category | flops | bytes accessed | tf_op | source)
XLA Modules:
  0.0 471.2 jit_solution(2877582283976164522)
XLA Ops:
  10.4 11.8 %all-to-all-start.1 = ((f32[1,32,8]{1,0,2:T(1,128)}), f32[1,32,8]{1,0,2:T(1,128)S(1)}, u32[]{:S(2)}, u32[]{:S(2)}) async-start(f32[1,32,8]{1,0,2:T(1,128)} %broadcast_in_dim.210), calls=%async_computation.1 | async-start | bytes 8192 | tf_op jit(solution)/shard_map/all_to_all | solution.py:124
  26.7 5.6 %all-to-all-done.1 = f32[1,32,8]{1,0,2:T(1,128)S(1)} async-done(((f32[1,32,8]{1,0,2:T(1,128)}), f32[1,32,8]{1,0,2:T(1,128)S(1)}, u32[]{:S(2)}, u32[]{:S(2)}) %all-to-all-start.1) | async-done | bytes 1056 | tf_op jit(solution)/shard_map/all_to_all | solution.py:124
  32.3 4.0 all-to-all-start
  37.5 29.1 %all-to-all-done = f32[1,32,64,128]{3,1,0,2:T(8,128)S(1)} async-done(((f32[1,32,64,128]{3,1,0,2:T(8,128)}), f32[1,32,64,128]{3,1,0,2:T(8,128)S(1)}, u32[]{:S(2)}, u32[]{:S(2)}) %all-to-all-start) | async-done | bytes 1048608 | tf_op jit(solution)/shard_map/all_to_all | solution.py:125
  68.3 4.2 all-to-all-start.3
  76.8 16.8 %all-gather = f32[8,1,32,1]{2,3,1,0:T(1,128)S(1)} all-gather(f32[1,1,32,1]{2,3,1,0:T(1,128)S(1)} %get-tuple-element.1929), channel_id=2, replica_groups=mesh['gx_0'=4,'gx_1'=2,'gy'=8,'gz_0'=4,'gz_1'=2] {'gy'}, dimensions={0}, use_global_device_ids=true | all-gather | bytes 1152 | tf_op jit(solution)/shard_map/all_gather | solution.py:24
  95.4 8.2 %all-gather.14 = f32[4,1,32]{2,1,0:T(1,128)S(1)} all-gather(f32[1,1,32]{2,1,0:T(1,128)S(1)} %get-tuple-element.1949), channel_id=1, replica_groups=mesh['gx_0'=4,'gx_1'=2,'gy'=8,'gz_0'=4,'gz_1'=2] {'gx_0'}, dimensions={0}, use_global_device_ids=true | all-gather | bytes 640 | tf_op jit(solution)/shard_map/all_gather | solution.py:24
  110.0 16.5 %all_gather.110 = f32[4,32,8,128]{3,2,1,0:T(8,128)S(1)} all-gather(f32[1,32,8,128]{3,2,1,0:T(8,128)S(1)} %slice_add_fusion.4), channel_id=1, replica_groups=mesh['gx_0'=4,'gx_1'=2,'gy'=8,'gz_0'=4,'gz_1'=2] {'gx_0'}, dimensions={0}, use_global_device_ids=true | all-gather | bytes 655360 | tf_op jit(solution)/shard_map/all_gather | solution.py:24
  134.1 6.5 %all-to-all-start.2 = ((f32[8,32,8,128]{3,2,1,0:T(8,128)}), f32[8,32,8,128]{3,2,1,0:T(8,128)}, u32[]{:S(2)}, u32[]{:S(2)}) async-start(f32[8,32,8,128]{3,2,1,0:T(8,128)} %constant_dynamic-update-slice_fusion.3), calls=%async_computation.2 | async-start | bytes 2097152 | tf_op jit(solution)/shard_map/all_to_all | solution.py:147
  145.8 57.4 %while.75 = (s32[]{:T(128)}, f32[4,256,8]{1,2,0:T(8,128)}, f32[4,8]{1,0:T(4,128)}, f32[4,1,8]{2,1,0:T(1,128)}, f32[4,256,8]{1,2,0:T(8,128)}, /*index=5*/f32[4,8,...) while((s32[]{:T(128)}, f32[4,256,8]{1,2,0:T(8,128)}, ...), condition=%wide.region_5.6_spmd.clone.clone, body=%wide.region_2.5_spmd.clone.clone.sunk | while | flops 3090474 | bytes 14180141 | solution.py:75
  147.4 4.2 multiply_dynamic-update-slice_fusion.4
  161.8 4.0 multiply_dynamic-update-slice_fusion.4
  176.1 4.2 multiply_dynamic-update-slice_fusion.4
  190.5 4.0 multiply_dynamic-update-slice_fusion.4
  224.4 157.7 %while.76 = (s32[]{:T(128)}, f32[256,256]{1,0:T(8,128)S(1)}, f32[256,128]{1,0:T(8,128)}, bf16[4,256,8,64]{1,3,2,0:T(8,128)(2,1)}, f32[4,256,8]{1,2,0:T(8,128)}, ...) while((s32[]{:T(128)}, f32[256,256]{1,0:T(8,128)S(1)}, ...), condition=%wide.region_19.20_spmd.clone.clone, body=%wide.region_6.19_spmd.clone.clone.sunk | while | flops 1215725568 | bytes 18326480 | solution.py:75
  229.8 6.5 %fusion.150 = (f32[8,256]{1,0:T(8,128)}, f32[8,256]{1,0:T(8,128)}, f32[256,256]{1,0:T(8,128)S(1)}, f32[8,256]{1,0:T(8,128)}) fusion(f32[4,8,256,256]{3,2,1,0:T(8,128)} %get-tuple-element.2535, s32[]{:T(128)S(6)} %sub.146, f32[256,256]{1,0:T(8,128)S(1)} %bitcast.583, f32[8,256]{1,0:T(8,128)S(1)} %dynamic-slice_bitcast_fusion.6, ...), kind=kOutput, calls=%fused_computation.87.clone.1 | convolution fusion | flops 408348672 | bytes 7964160 | tf_op jit(solution)/shard_map/transpose(jvp())/while/body/eval_jaxpr/hts,shp->thp/dot_general | solution.py:50
  241.4 3.2 reduce-window.62
  254.5 3.7 fusion.154
  269.2 6.5 %fusion.150 = (f32[8,256]{1,0:T(8,128)}, f32[8,256]{1,0:T(8,128)}, f32[256,256]{1,0:T(8,128)S(1)}, f32[8,256]{1,0:T(8,128)}) fusion(f32[4,8,256,256]{3,2,1,0:T(8,128)} %get-tuple-element.2535, s32[]{:T(128)S(6)} %sub.146, f32[256,256]{1,0:T(8,128)S(1)} %bitcast.583, f32[8,256]{1,0:T(8,128)S(1)} %dynamic-slice_bitcast_fusion.6, ...), kind=kOutput, calls=%fused_computation.87.clone.1 | convolution fusion | flops 408348672 | bytes 7964160 | tf_op jit(solution)/shard_map/transpose(jvp())/while/body/eval_jaxpr/hts,shp->thp/dot_general | solution.py:50
  280.8 3.2 reduce-window.62
  293.9 3.7 fusion.154
  308.6 6.5 %fusion.150 = (f32[8,256]{1,0:T(8,128)}, f32[8,256]{1,0:T(8,128)}, f32[256,256]{1,0:T(8,128)S(1)}, f32[8,256]{1,0:T(8,128)}) fusion(f32[4,8,256,256]{3,2,1,0:T(8,128)} %get-tuple-element.2535, s32[]{:T(128)S(6)} %sub.146, f32[256,256]{1,0:T(8,128)S(1)} %bitcast.583, f32[8,256]{1,0:T(8,128)S(1)} %dynamic-slice_bitcast_fusion.6, ...), kind=kOutput, calls=%fused_computation.87.clone.1 | convolution fusion | flops 408348672 | bytes 7964160 | tf_op jit(solution)/shard_map/transpose(jvp())/while/body/eval_jaxpr/hts,shp->thp/dot_general | solution.py:50
  320.2 3.2 reduce-window.62
  333.3 3.7 fusion.154
  348.0 6.5 %fusion.150 = (f32[8,256]{1,0:T(8,128)}, f32[8,256]{1,0:T(8,128)}, f32[256,256]{1,0:T(8,128)S(1)}, f32[8,256]{1,0:T(8,128)}) fusion(f32[4,8,256,256]{3,2,1,0:T(8,128)} %get-tuple-element.2535, s32[]{:T(128)S(6)} %sub.146, f32[256,256]{1,0:T(8,128)S(1)} %bitcast.583, f32[8,256]{1,0:T(8,128)S(1)} %dynamic-slice_bitcast_fusion.6, ...), kind=kOutput, calls=%fused_computation.87.clone.1 | convolution fusion | flops 408348672 | bytes 7964160 | tf_op jit(solution)/shard_map/transpose(jvp())/while/body/eval_jaxpr/hts,shp->thp/dot_general | solution.py:50
  372.7 3.7 fusion.154
  383.0 10.8 %all-gather.15 = f32[4,1,32]{2,1,0:T(1,128)S(1)} all-gather(f32[1,1,32]{2,1,0:T(1,128)S(1)} %reshape.982), channel_id=1, replica_groups=mesh['gx_0'=4,'gx_1'=2,'gy'=8,'gz_0'=4,'gz_1'=2] {'gx_0'}, dimensions={0}, use_global_device_ids=true | all-gather | bytes 640 | tf_op jit(solution)/shard_map/all_gather | solution.py:36
  394.6 8.3 %all-gather.16 = f32[4,1,32]{2,1,0:T(1,128)S(1)} all-gather(f32[1,1,32]{2,1,0:T(1,128)S(1)} %reshape.984), channel_id=1, replica_groups=mesh['gx_0'=4,'gx_1'=2,'gy'=8,'gz_0'=4,'gz_1'=2] {'gx_0'}, dimensions={0}, use_global_device_ids=true | all-gather | bytes 640 | tf_op jit(solution)/shard_map/all_gather | solution.py:36
  403.6 9.1 %all-gather.17 = f32[4,1,32]{2,1,0:T(1,128)S(1)} all-gather(f32[1,1,32]{2,1,0:T(1,128)S(1)} %reshape.986), channel_id=1, replica_groups=mesh['gx_0'=4,'gx_1'=2,'gy'=8,'gz_0'=4,'gz_1'=2] {'gx_0'}, dimensions={0}, use_global_device_ids=true | all-gather | bytes 640 | tf_op jit(solution)/shard_map/all_gather | solution.py:36
  416.9 16.1 %all-reduce.14 = (f32[256]{0:T(256)S(1)}, f32[256]{0:T(256)S(1)}, f32[256]{0:T(256)S(1)}) all-reduce(f32[256]{0:T(256)S(1)} %dynamic-update-slice.1, f32[256]{0:T(256)S(1)} %dynamic-update-slice.5, f32[256]{0:T(256)S(1)} %dynamic-update-slice.9), channel_id=4, replica_groups=mesh['gx_0'=4,'gx_1'=2,'gy'=8,'gz_0'=4,'gz_1'=2] {'gy'}, use_global_device_ids=true, to_apply=%add.3 | all-reduce | flops 768 | bytes 6144
  433.9 10.9 %all-reduce.15 = (f32[128]{0:T(128)S(1)}, f32[128]{0:T(128)S(1)}, f32[128]{0:T(128)S(1)}) all-reduce(f32[128]{0:T(128)S(1)} %dynamic-update-slice.2, f32[128]{0:T(128)S(1)} %dynamic-update-slice.6, f32[128]{0:T(128)S(1)} %dynamic-update-slice.10), channel_id=5, replica_groups=mesh['gx_0'=4,'gx_1'=2,'gy'=8,'gz_0'=4,'gz_1'=2] {'gz_0'}, use_global_device_ids=true, to_apply=%add.4 | all-reduce | flops 384 | bytes 3072
  445.9 8.8 %all-reduce.16 = (f32[64]{0:T(128)S(1)}, f32[64]{0:T(128)S(1)}, f32[64]{0:T(128)S(1)}) all-reduce(f32[64]{0:T(128)S(1)} %dynamic-update-slice.3, f32[64]{0:T(128)S(1)} %dynamic-update-slice.7, f32[64]{0:T(128)S(1)} %dynamic-update-slice.11), channel_id=6, replica_groups=mesh['gx_0'=4,'gx_1'=2,'gy'=8,'gz_0'=4,'gz_1'=2] {'gz_1'}, use_global_device_ids=true, to_apply=%add.5 | all-reduce | flops 192 | bytes 1536
  (429 shorter events, 220.4 us)
Async XLA Ops:
  7.2 16.8 %copy-start = (bf16[256,128]{1,0:T(8,128)(2,1)S(1)}, bf16[256,128]{1,0:T(8,128)(2,1)}, u32[]{:S(2)}) copy-start(bf16[256,128]{1,0:T(8,128)(2,1)} %param.16) | copy-start | bytes 196612
  10.4 21.9 %all-to-all-start.1 = ((f32[1,32,8]{1,0,2:T(1,128)}), f32[1,32,8]{1,0,2:T(1,128)S(1)}, u32[]{:S(2)}, u32[]{:S(2)}) async-start(f32[1,32,8]{1,0,2:T(1,128)} %broadcast_in_dim.210), calls=%async_computation.1 | async-start | bytes 8192 | tf_op jit(solution)/shard_map/all_to_all | solution.py:124
  32.3 34.3 %all-to-all-start = ((f32[1,32,64,128]{3,1,0,2:T(8,128)}), f32[1,32,64,128]{3,1,0,2:T(8,128)S(1)}, u32[]{:S(2)}, u32[]{:S(2)}) async-start(f32[1,32,64,128]{3,1,0,2:T(8,128)} %copy.195), calls=%async_computation | async-start | bytes 2097152 | tf_op jit(solution)/shard_map/all_to_all | solution.py:125
  36.3 69.5 %all-gather.20.cloned.1.call-start = ((), (), s32[]{:S(2)}) async-start(), calls=%async_computation.4 | async-start | bytes 1179648 | tf_op jit(solution)/shard_map/all_gather | solution.py:24
  37.0 31.3 %copy-start.18 = (f32[32]{0:T(128)}, f32[32]{0:T(128)S(1)}, u32[]{:S(2)}) copy-start(f32[32]{0:T(128)S(1)} %get-tuple-element.1944) | copy-start | bytes 388
  37.4 30.9 %copy-start.20 = (f32[32]{0:T(128)}, f32[32]{0:T(128)S(1)}, u32[]{:S(2)}) copy-start(f32[32]{0:T(128)S(1)} %get-tuple-element.1935) | copy-start | bytes 388
  37.4 30.9 %copy-start.22 = (f32[32]{0:T(128)}, f32[32]{0:T(128)S(1)}, u32[]{:S(2)}) copy-start(f32[32]{0:T(128)S(1)} %get-tuple-element.1931) | copy-start | bytes 388
  37.4 30.9 %copy-start.24 = (f32[32]{0:T(128)}, f32[32]{0:T(128)S(1)}, u32[]{:S(2)}) copy-start(f32[32]{0:T(128)S(1)} %get-tuple-element.1933) | copy-start | bytes 388
  37.4 35.2 %copy-start.31 = (f32[32]{0:T(128)S(1)}, f32[32]{0:T(128)}, u32[]{:S(2)}) copy-start(f32[32]{0:T(128)} %param.18) | copy-start | bytes 388
  37.5 35.8 %copy-start.41 = (f32[32]{0:T(128)S(1)}, f32[32]{0:T(128)}, u32[]{:S(2)}) copy-start(f32[32]{0:T(128)} %param.17) | copy-start | bytes 388
  68.3 65.7 %all-to-all-start.3 = ((bf16[8,32,8,128]{3,2,1,0:T(8,128)(2,1)}), bf16[8,32,8,128]{3,2,1,0:T(8,128)(2,1)}, u32[]{:S(2)}, u32[]{:S(2)}) async-start(bf16[8,32,8,128]{3,2,1,0:T(8,128)(2,1)} %param.20), calls=%async_computation.3 | async-start | bytes 1048576 | tf_op jit(solution)/shard_map/all_to_all | solution.py:106
  93.6 14.0 %copy-start.15 = (f32[32]{0:T(128)}, f32[32]{0:T(128)S(1)}, u32[]{:S(2)}) copy-start(f32[32]{0:T(128)S(1)} %get-tuple-element.1940) | copy-start | bytes 388
  93.6 14.0 %copy-start.16 = (f32[32]{0:T(128)}, f32[32]{0:T(128)S(1)}, u32[]{:S(2)}) copy-start(f32[32]{0:T(128)S(1)} %get-tuple-element.1942) | copy-start | bytes 388
  95.4 14.4 %copy-start.21 = (f32[32]{0:T(128)}, f32[32]{0:T(128)S(1)}, u32[]{:S(2)}) copy-start(f32[32]{0:T(128)S(1)} %get-tuple-element.1950) | copy-start | bytes 388
  105.8 20.7 %copy-start.5 = (f32[8,32,8,128]{3,2,1,0:T(8,128)S(1)}, f32[8,32,8,128]{3,2,1,0:T(8,128)}, u32[]{:S(2)}) copy-start(f32[8,32,8,128]{3,2,1,0:T(8,128)} %all-gather.20.cloned.1.call-done) | copy-start | bytes 3145732
  105.8 20.7 %copy-start.33 = (f32[32]{0:T(128)S(1)}, f32[32]{0:T(128)}, u32[]{:S(2)}) copy-start(f32[32]{0:T(128)} %get-tuple-element.1905) | copy-start | bytes 388
  105.8 20.7 %copy-start.34 = (f32[32]{0:T(128)S(1)}, f32[32]{0:T(128)}, u32[]{:S(2)}) copy-start(f32[32]{0:T(128)} %get-tuple-element.1906) | copy-start | bytes 388
  105.8 20.7 %copy-start.35 = (f32[32]{0:T(128)S(1)}, f32[32]{0:T(128)}, u32[]{:S(2)}) copy-start(f32[32]{0:T(128)} %get-tuple-element.1945) | copy-start | bytes 388
  105.8 20.7 %copy-start.36 = (f32[32]{0:T(128)S(1)}, f32[32]{0:T(128)}, u32[]{:S(2)}) copy-start(f32[32]{0:T(128)} %get-tuple-element.1946) | copy-start | bytes 388
  105.8 20.7 %copy-start.37 = (f32[32]{0:T(128)S(1)}, f32[32]{0:T(128)}, u32[]{:S(2)}) copy-start(f32[32]{0:T(128)} %get-tuple-element.1947) | copy-start | bytes 388
  105.9 20.7 %copy-start.38 = (f32[32]{0:T(128)S(1)}, f32[32]{0:T(128)}, u32[]{:S(2)}) copy-start(f32[32]{0:T(128)} %get-tuple-element.1948) | copy-start | bytes 388
  107.6 21.2 %copy-start.30 = (f32[32]{0:T(128)S(1)}, f32[32]{0:T(128)}, u32[]{:S(2)}) copy-start(f32[32]{0:T(128)} %get-tuple-element.1900) | copy-start | bytes 388
  107.6 21.9 %copy-start.7 = (f32[1,32,8,128]{3,2,1,0:T(8,128)S(1)}, f32[1,32,8,128]{3,2,1,0:T(8,128)}, u32[]{:S(2)}) copy-start(f32[1,32,8,128]{3,2,1,0:T(8,128)} %get-tuple-element.1911) | copy-start | bytes 393220
  107.6 21.9 %copy-start.25 = (f32[32]{0:T(128)S(1)}, f32[32]{0:T(128)}, u32[]{:S(2)}) copy-start(f32[32]{0:T(128)} %copy-done.24) | copy-start | bytes 388
  107.7 21.9 %copy-start.40 = (f32[32]{0:T(128)S(1)}, f32[32]{0:T(128)}, u32[]{:S(2)}) copy-start(f32[32]{0:T(128)} %get-tuple-element.1901) | copy-start | bytes 388
  109.8 20.5 %copy-start.29 = (f32[32]{0:T(128)S(1)}, f32[32]{0:T(128)}, u32[]{:S(2)}) copy-start(f32[32]{0:T(128)} %get-tuple-element.1902) | copy-start | bytes 388
  109.9 21.2 %copy-start.6 = (f32[1,32,8,128]{3,2,1,0:T(8,128)S(1)}, f32[1,32,8,128]{3,2,1,0:T(8,128)}, u32[]{:S(2)}) copy-start(f32[1,32,8,128]{3,2,1,0:T(8,128)} %get-tuple-element.1912) | copy-start | bytes 393220
  109.9 21.1 %copy-start.23 = (f32[32]{0:T(128)S(1)}, f32[32]{0:T(128)}, u32[]{:S(2)}) copy-start(f32[32]{0:T(128)} %copy-done.22) | copy-start | bytes 388
  110.0 21.1 %copy-start.39 = (f32[32]{0:T(128)S(1)}, f32[32]{0:T(128)}, u32[]{:S(2)}) copy-start(f32[32]{0:T(128)} %get-tuple-element.1903) | copy-start | bytes 388
  134.1 84.2 %all-to-all-start.2 = ((f32[8,32,8,128]{3,2,1,0:T(8,128)}), f32[8,32,8,128]{3,2,1,0:T(8,128)}, u32[]{:S(2)}, u32[]{:S(2)}) async-start(f32[8,32,8,128]{3,2,1,0:T(8,128)} %constant_dynamic-update-slice_fusion.3), calls=%async_computation.2 | async-start | bytes 2097152 | tf_op jit(solution)/shard_map/all_to_all | solution.py:147
  382.1 79.7 %copy-start.2 = (f32[4,256,8,64]{1,3,2,0:T(8,128)S(1)}, f32[4,256,8,64]{1,3,2,0:T(8,128)}, u32[]{:S(2)}) copy-start(f32[4,256,8,64]{1,3,2,0:T(8,128)} %get-tuple-element.1033) | copy-start | bytes 6291460
  382.1 79.7 %copy-start.4 = (bf16[8,32,8,128]{3,2,0,1:T(8,128)(2,1)S(1)}, bf16[8,32,8,128]{3,2,0,1:T(8,128)(2,1)}, u32[]{:S(2)}) copy-start(bf16[8,32,8,128]{3,2,0,1:T(8,128)(2,1)} %copy-done.3) | copy-start | bytes 1572868
  (25 other events, 129.1 us)
Sparse Core Ops, SparseCore 0:
  68.4 37.3 all-gather.19
